TPU v7x, 32 devices: a whole 2x2x4 slice. The times are simulated.
32 devices in a mesh: image: 4 (over y, x), band: 2 (over core), ga: 4 (over z).
Axes of the slice: x: 2, y: 2, z: 4, core: 2. Of those that a mesh axis runs over, the one named last changes fastest.
Arguments:
- wave_coeffs: bfloat16 [4, 64, 2, 262144], P('image', 'band', None, 'ga'), may hold values from -6 to 6
- occupation: float32 [4, 64], P('image', 'band'), may hold values from 0.003125 to 0.0625
- form_factor: float32 [4, 8, 262144], P(None, None, 'ga'), may hold values from -0.005859375 to 0.005859375
- g_vectors: float32 [3, 262144], P(None, 'ga'), may hold values from -2 to 2
- species: int32 [64], replicated, may hold values from 0 to 3
- proj_count: int32 [4], replicated, may hold values from 1 to 8, as said below
- coupling: float32 [4, 8], replicated, may hold values from 0.5 to 2.5
- positions: float32 [4, 3, 64], P('image'), may hold values from -5.4 to 29.4, as said below
- energy_rest: float32 [4], P('image'), may hold values from -8 to 8
- force_rest: float32 [4, 3, 64], P('image'), may hold values from -6 to 6
- end_positions: float32 [2, 3, 64], replicated, may hold values from -5.4 to 29.4, as said below
- end_energy: float32 [2], replicated, may hold values from -8 to 8
- climb_index: int32 [1], replicated, may hold values from 0 to 3
- tangent_kind: int32 [4], P('image'), may hold values from 0 to 3
Outputs:
- neb_force: float32 [4, 3, 64], P('image')
- energy: float32 [4], P('image')
Inputs may be any that keep to these rules, and one draw needn't show every extreme that they name: `proj_count`: each species has between 1 and 8 live projector slots, and some species has exactly 8. `positions`: atom coordinates in bohr. `end_positions`: atom coordinates in bohr.
All inputs are finite; a program needn't handle non-finite values.
Results may differ from a plain program's by a relative error of at most 0.0003.
The roundings to bfloat16 on the way count: a program that leaves them out, or rounds other values in their place, can miss the bound.
Values sent between devices are 32-bit elements; how exact they have to be, the bound alone decides.
A program may use at most 128 MiB of HBM per device.

v0:
```python
import math

import jax
import jax.numpy as jnp
from jax import lax
from jax.sharding import PartitionSpec as P

ATOMS = 64
PMAX = 8
SPECIES = 4


spring_constant = 5.0


def passed_along(array, axis, by):
    length = lax.axis_size(axis)
    pairs = [(i, i + by) for i in range(length) if 0 <= i + by < length]
    return lax.ppermute(array, axis, pairs)


def atom_tables(species, proj_count, coupling):
    is_species = (species[:, None] == jnp.arange(SPECIES)[None, :]).astype(jnp.float32)
    is_live = (jnp.arange(PMAX)[None, :] < proj_count[:, None]).astype(jnp.float32)
    species_mask = is_species[:, :, None] * is_live[None, :, :]
    strength = jnp.sum(species_mask * coupling[None, :, :], axis=1)
    return (species_mask, strength)


def projectors(atom_pos, species_mask, form_factor, g_vectors):
    phases = atom_pos[0][:, None] * g_vectors[0][None, :]
    phases = phases + atom_pos[1][:, None] * g_vectors[1][None, :]
    phases = phases + atom_pos[2][:, None] * g_vectors[2][None, :]
    cosine = jnp.cos(phases)
    sine_part = jnp.sin(phases)
    radial = species_mask[:, 0, :, None] * form_factor[0][None, :, :]
    for spec_num in range(1, SPECIES):
        radial = radial + species_mask[:, spec_num, :, None] * form_factor[spec_num][None, :, :]
    real_part = radial * cosine[:, None, :]
    imag_part = -radial * sine_part[:, None, :]
    joined = jnp.concatenate([real_part, imag_part], axis=-1).astype(jnp.bfloat16)
    return joined.reshape(joined.shape[0] * joined.shape[1], joined.shape[2])


def stack_waves(waves_here, g_vectors):
    band_count = waves_here.shape[0]
    real_part = waves_here[:, 0, :].astype(jnp.float32)
    imag_part = waves_here[:, 1, :].astype(jnp.float32)
    pieces = [waves_here.reshape(band_count, 2 * waves_here.shape[2])]
    for axis_num in range(3):
        direction = g_vectors[axis_num][None, :]
        pieces.append(
            jnp.concatenate([-direction * imag_part, direction * real_part], axis=-1).astype(
                jnp.bfloat16
            )
        )
    return jnp.concatenate(pieces, axis=0)


def contract(projector, stacked):
    return 2.0 * lax.dot_general(
        projector, stacked, (((1,), (1,)), ((), ())), preferred_element_type=jnp.float32
    )


def nonlocal_terms(proj_sums, occupied, strength):
    band_count = occupied.shape[0]
    atom_count = strength.shape[0]
    intersect = proj_sums[:, :band_count]
    weighted = intersect * occupied[None, :]
    energy_part = jnp.sum(strength.reshape(-1) * jnp.sum(weighted * intersect, axis=1))
    forces = []
    for axis_num in range(3):
        slope = proj_sums[:, (axis_num + 1) * band_count : (axis_num + 2) * band_count]
        per_row = jnp.sum(weighted * slope, axis=1).reshape(atom_count, PMAX)
        forces.append(-2.0 * jnp.sum(strength * per_row, axis=1))
    return (energy_part, jnp.stack(forces, axis=0))


def neb_project(
    force, here, prev_pos, next_pos, energy, prev_energy, next_energy, tangent_kind, is_climb
):
    to_next = next_pos - here
    from_prev = here - prev_pos
    rise_next = jnp.abs(next_energy - energy)
    rise_prev = jnp.abs(prev_energy - energy)
    larger = jnp.maximum(rise_next, rise_prev)
    smaller = jnp.minimum(rise_next, rise_prev)
    rising = next_energy > prev_energy
    weight_next = 1.0 + jnp.where(rising, larger, smaller)
    weight_prev = 1.0 + jnp.where(rising, smaller, larger)
    stiff_next = spring_constant * (1.0 + jax.nn.sigmoid(0.5 * (next_energy + energy)))
    stiff_prev = spring_constant * (1.0 + jax.nn.sigmoid(0.5 * (prev_energy + energy)))
    length_next = jnp.sqrt(jnp.sum(to_next * to_next, axis=(1, 2)) + 1.0)
    length_prev = jnp.sqrt(jnp.sum(from_prev * from_prev, axis=(1, 2)) + 1.0)
    upwind = weight_next[:, None, None] * to_next + weight_prev[:, None, None] * from_prev
    forward = to_next / length_next[:, None, None]
    backward = from_prev / length_prev[:, None, None]
    kind = tangent_kind[:, None, None]
    tangent = jnp.where(
        kind == 0,
        upwind,
        jnp.where(kind == 1, forward + backward, jnp.where(kind == 2, forward, backward)),
    )
    unit_tangent = tangent / jnp.sqrt(jnp.sum(tangent * tangent, axis=(1, 2)) + 1.0)[:, None, None]
    along = jnp.sum(force * unit_tangent, axis=(1, 2))[:, None, None]
    climbing = force - 2.0 * along * unit_tangent
    regular = (
        force
        - along * unit_tangent
        + (stiff_next * length_next - stiff_prev * length_prev)[:, None, None] * unit_tangent
    )
    return jnp.where(is_climb[:, None, None], climbing, regular)


def per_device(
    wave_coeffs,
    occupation,
    form_factor,
    g_vectors,
    species,
    proj_count,
    coupling,
    positions,
    energy_rest,
    force_rest,
    end_positions,
    end_energy,
    climb_index,
    tangent_kind,
):
    species_mask, strength = atom_tables(species, proj_count, coupling)
    stacked = stack_waves(wave_coeffs[0], g_vectors)
    atom_pos = positions[0]
    occupied = occupation[0]
    local_atoms = ATOMS // lax.axis_size("ga")
    natoms = lax.axis_size("ga") * (local_atoms * PMAX) // PMAX
    block_atoms = math.gcd(natoms, 8)
    block_count = natoms // block_atoms

    def one_block(block_num):
        begin = block_num * block_atoms
        pos_part = lax.dynamic_slice_in_dim(atom_pos, begin, block_atoms, 1)
        mask_part = lax.dynamic_slice_in_dim(species_mask, begin, block_atoms, 0)
        projector = projectors(pos_part, mask_part, form_factor, g_vectors)
        return contract(projector, stacked)

    blocks = lax.map(one_block, jnp.arange(block_count, dtype=jnp.int32))
    proj_sums = lax.psum_scatter(
        blocks.reshape(lax.axis_size("ga") * (local_atoms * PMAX), blocks.shape[2]),
        "ga",
        scatter_dimension=0,
        tiled=True,
    )
    first_local = lax.axis_index("ga") * local_atoms
    strength_part = lax.dynamic_slice_in_dim(strength, first_local, local_atoms, 0)
    energy_part, force_part = nonlocal_terms(proj_sums, occupied, strength_part)
    force_full = lax.dynamic_update_slice_in_dim(
        jnp.zeros((3, ATOMS), jnp.float32), force_part, first_local, 1
    )
    force_nl, energy_nl = lax.psum((force_full, energy_part), ("band", "ga"))
    energy = energy_rest + energy_nl
    force = force_rest + force_nl[None, :, :]
    image_index = lax.axis_index("image")
    image_count = lax.axis_size("image")
    prev_pos, prev_energy = passed_along((positions, energy), "image", 1)
    next_pos, next_energy = passed_along((positions, energy), "image", -1)
    at_start = image_index == 0
    at_end = image_index == image_count - 1
    prev_pos = jnp.where(at_start, end_positions[:1], prev_pos)
    prev_energy = jnp.where(at_start, end_energy[:1], prev_energy)
    next_pos = jnp.where(at_end, end_positions[1:], next_pos)
    next_energy = jnp.where(at_end, end_energy[1:], next_energy)
    is_climb = climb_index == image_index
    neb_force = neb_project(
        force,
        positions,
        prev_pos,
        next_pos,
        energy,
        prev_energy,
        next_energy,
        tangent_kind,
        is_climb,
    )
    return (neb_force, energy)


def solution(mesh):
    in_specs = (
        P("image", "band", None, "ga"),
        P("image", "band"),
        P(None, None, "ga"),
        P(None, "ga"),
        P(),
        P(),
        P(),
        P("image", None, None),
        P("image"),
        P("image", None, None),
        P(),
        P(),
        P(),
        P("image"),
    )
    out_specs = (P("image", None, None), P("image"))
    return jax.shard_map(
        per_device, mesh=mesh, in_specs=in_specs, out_specs=out_specs, check_vma=False
    )
```

profile of v0, /device:TPU:10, one launch (start us, length us, event | category | flops | bytes accessed | tf_op | source)
XLA Modules:
  0.0 495.8 jit_solution(12837943678773757339)
XLA Ops:
  7.2 3.3 slice_negate_fusion.2
  10.5 11.2 %copy.24 = bf16[1,32,2,65536]{3,1,2,0:T(8,128)(2,1)} copy(bf16[1,32,2,65536]{3,2,1,0:T(2,128)(2,1)} %param.16) | data formatting | bytes 16777216 | tf_op args[0]
  21.7 11.2 %copy.21 = bf16[4,8,2,65536]{3,1,2,0:T(8,128)(2,1)} copy(bf16[4,8,2,65536]{3,2,1,0:T(2,128)(2,1)} %bitcast.165) | data formatting | bytes 16777216
  33.7 11.5 %fusion.22 = (bf16[32,65536]{1,0:T(8,128)(2,1)}, bf16[32,65536]{1,0:T(8,128)(2,1)}, bf16[32,65536]{1,0:T(8,128)(2,1)}, bf16[32,65536]{1,0:T(8,128)(2,1)}, bf16[3...) fusion(f32[65536]{0:T(1024)S(1)} %bitcast.171, bf16[32,2,65536]{2,0,1:T(8,128)(2,1)} %bitcast.166, f32[65536]{0:T(1024)S(1)} %bitcast.176, ...), kind=kLoop, calls=%fused_computation.42 | loop fusion | flops 29360128 | bytes 35127296 | tf_op jit(solution)/shard_map/convert.8
  45.3 32.5 %maximum_maximum_fusion = bf16[128,131072]{1,0:T(8,128)(2,1)} fusion(bf16[32,65536]{1,0:T(8,128)(2,1)} %get-tuple-element.99, bf16[32,65536]{1,0:T(8,128)(2,1)} %get-tuple-element.101, bf16[32,65536]{1,0:T(8,128)(2,1)} %get-tuple-element.100, bf16[32,65536]{1,0:T(8,128)(2,1)} %get-tuple-element.102, bf16[32,65536]{1,0:T(8,128)(2,1)} %get-tuple-element.103, ...), kind=kLoop, calls=%fused_computation.35 | loop fusion | flops 234881024 | bytes 67108864 | tf_op jit(solution)/shard_map/concatenate | solution.py:57
  77.8 351.9 %while.10 = (s32[]{:T(128)}, f32[8,64,128]{2,1,0:T(8,128)S(1)}, s32[8]{0:T(128)S(1)}, f32[64,4,8]{2,0,1:T(8,128)S(1)}, f32[4,8,65536]{2,1,0:T(8,128)}, /*index=5...) while((s32[]{:T(128)}, f32[8,64,128]{2,1,0:T(8,128)S(1)}, ...), condition=%wide.region_2.3_spmd, body=%wide.region_1.2_spmd.sunk | while | flops 2233999360 | bytes 111457432 | solution.py:148
  79.7 8.6 %fusion.50 = (f32[8,65536]{1,0:T(8,128)S(1)}, f32[8,65536]{1,0:T(8,128)}) fusion(f32[65536]{0:T(1024)S(1)} %bitcast.169, f32[8]{0:T(128)S(1)} %get-tuple-element.186, f32[65536]{0:T(1024)S(1)} %bitcast.170, f32[8]{0:T(128)S(1)} %get-tuple-element.188, f32[65536]{0:T(1024)S(1)} %bitcast.168, f32[8]{0:T(128)S(1)} %get-tuple-element.190), kind=kLoop, calls=%fused_computation.18.clone.1 | loop fusion | flops 2621440 | bytes 4980832 | tf_op jit(solution)/shard_map/while/body/eval_jaxpr/cos | solution.py:34
  89.2 4.2 slice_bitcast_fusion.12
  93.4 8.9 %fusion.51 = (bf16[64,65536]{1,0:T(8,128)(2,1)}, bf16[64,65536]{1,0:T(8,128)(2,1)}) fusion(f32[8,65536]{1,0:T(8,128)S(1)} %get-tuple-element.191, f32[8,65536]{1,0:T(8,128)S(1)} %get-tuple-element.192, f32[64]{0:T(128)S(1)} %copy-done.5, f32[8,65536]{1,0:T(8,128)S(1)} %get-tuple-element.194, f32[64]{0:T(128)S(1)} %mul.729, ...), kind=kLoop, calls=%fused_computation.7.clone.1 | loop fusion | flops 50331648 | bytes 29361152 | tf_op jit(solution)/shard_map/convert
  102.3 19.5 %fusion.52 = f32[8,64,128]{2,1,0:T(8,128)S(1)} fusion(f32[8,64,128]{2,1,0:T(8,128)S(1)} %get-tuple-element.219, s32[]{:T(128)} %get-tuple-element.218, bf16[128,131072]{1,0:T(8,128)(2,1)} %get-tuple-element.240, bf16[64,65536]{1,0:T(8,128)(2,1)} %get-tuple-element.201, bf16[64,65536]{1,0:T(8,128)(2,1)} %get-tuple-element.202), kind=kOutput, calls=%fused_computation.25.clone.1 | convolution fusion | flops 2181046272 | bytes 50364420 | tf_op jit(solution)/shard_map/while/body/eval_jaxpr/dot_general | solution.py:61
  123.7 8.6 %fusion.50 = (f32[8,65536]{1,0:T(8,128)S(1)}, f32[8,65536]{1,0:T(8,128)}) fusion(f32[65536]{0:T(1024)S(1)} %bitcast.169, f32[8]{0:T(128)S(1)} %get-tuple-element.186, f32[65536]{0:T(1024)S(1)} %bitcast.170, f32[8]{0:T(128)S(1)} %get-tuple-element.188, f32[65536]{0:T(1024)S(1)} %bitcast.168, f32[8]{0:T(128)S(1)} %get-tuple-element.190), kind=kLoop, calls=%fused_computation.18.clone.1 | loop fusion | flops 2621440 | bytes 4980832 | tf_op jit(solution)/shard_map/while/body/eval_jaxpr/cos | solution.py:34
  133.2 4.2 slice_bitcast_fusion.12
  137.4 8.9 %fusion.51 = (bf16[64,65536]{1,0:T(8,128)(2,1)}, bf16[64,65536]{1,0:T(8,128)(2,1)}) fusion(f32[8,65536]{1,0:T(8,128)S(1)} %get-tuple-element.191, f32[8,65536]{1,0:T(8,128)S(1)} %get-tuple-element.192, f32[64]{0:T(128)S(1)} %copy-done.5, f32[8,65536]{1,0:T(8,128)S(1)} %get-tuple-element.194, f32[64]{0:T(128)S(1)} %mul.729, ...), kind=kLoop, calls=%fused_computation.7.clone.1 | loop fusion | flops 50331648 | bytes 29361152 | tf_op jit(solution)/shard_map/convert
  146.3 19.5 %fusion.52 = f32[8,64,128]{2,1,0:T(8,128)S(1)} fusion(f32[8,64,128]{2,1,0:T(8,128)S(1)} %get-tuple-element.219, s32[]{:T(128)} %get-tuple-element.218, bf16[128,131072]{1,0:T(8,128)(2,1)} %get-tuple-element.240, bf16[64,65536]{1,0:T(8,128)(2,1)} %get-tuple-element.201, bf16[64,65536]{1,0:T(8,128)(2,1)} %get-tuple-element.202), kind=kOutput, calls=%fused_computation.25.clone.1 | convolution fusion | flops 2181046272 | bytes 50364420 | tf_op jit(solution)/shard_map/while/body/eval_jaxpr/dot_general | solution.py:61
  167.7 8.6 %fusion.50 = (f32[8,65536]{1,0:T(8,128)S(1)}, f32[8,65536]{1,0:T(8,128)}) fusion(f32[65536]{0:T(1024)S(1)} %bitcast.169, f32[8]{0:T(128)S(1)} %get-tuple-element.186, f32[65536]{0:T(1024)S(1)} %bitcast.170, f32[8]{0:T(128)S(1)} %get-tuple-element.188, f32[65536]{0:T(1024)S(1)} %bitcast.168, f32[8]{0:T(128)S(1)} %get-tuple-element.190), kind=kLoop, calls=%fused_computation.18.clone.1 | loop fusion | flops 2621440 | bytes 4980832 | tf_op jit(solution)/shard_map/while/body/eval_jaxpr/cos | solution.py:34
  177.2 4.2 slice_bitcast_fusion.12
  181.4 8.9 %fusion.51 = (bf16[64,65536]{1,0:T(8,128)(2,1)}, bf16[64,65536]{1,0:T(8,128)(2,1)}) fusion(f32[8,65536]{1,0:T(8,128)S(1)} %get-tuple-element.191, f32[8,65536]{1,0:T(8,128)S(1)} %get-tuple-element.192, f32[64]{0:T(128)S(1)} %copy-done.5, f32[8,65536]{1,0:T(8,128)S(1)} %get-tuple-element.194, f32[64]{0:T(128)S(1)} %mul.729, ...), kind=kLoop, calls=%fused_computation.7.clone.1 | loop fusion | flops 50331648 | bytes 29361152 | tf_op jit(solution)/shard_map/convert
  190.3 19.5 %fusion.52 = f32[8,64,128]{2,1,0:T(8,128)S(1)} fusion(f32[8,64,128]{2,1,0:T(8,128)S(1)} %get-tuple-element.219, s32[]{:T(128)} %get-tuple-element.218, bf16[128,131072]{1,0:T(8,128)(2,1)} %get-tuple-element.240, bf16[64,65536]{1,0:T(8,128)(2,1)} %get-tuple-element.201, bf16[64,65536]{1,0:T(8,128)(2,1)} %get-tuple-element.202), kind=kOutput, calls=%fused_computation.25.clone.1 | convolution fusion | flops 2181046272 | bytes 50364420 | tf_op jit(solution)/shard_map/while/body/eval_jaxpr/dot_general | solution.py:61
  211.7 8.6 %fusion.50 = (f32[8,65536]{1,0:T(8,128)S(1)}, f32[8,65536]{1,0:T(8,128)}) fusion(f32[65536]{0:T(1024)S(1)} %bitcast.169, f32[8]{0:T(128)S(1)} %get-tuple-element.186, f32[65536]{0:T(1024)S(1)} %bitcast.170, f32[8]{0:T(128)S(1)} %get-tuple-element.188, f32[65536]{0:T(1024)S(1)} %bitcast.168, f32[8]{0:T(128)S(1)} %get-tuple-element.190), kind=kLoop, calls=%fused_computation.18.clone.1 | loop fusion | flops 2621440 | bytes 4980832 | tf_op jit(solution)/shard_map/while/body/eval_jaxpr/cos | solution.py:34
  221.2 4.2 slice_bitcast_fusion.12
  225.4 8.9 %fusion.51 = (bf16[64,65536]{1,0:T(8,128)(2,1)}, bf16[64,65536]{1,0:T(8,128)(2,1)}) fusion(f32[8,65536]{1,0:T(8,128)S(1)} %get-tuple-element.191, f32[8,65536]{1,0:T(8,128)S(1)} %get-tuple-element.192, f32[64]{0:T(128)S(1)} %copy-done.5, f32[8,65536]{1,0:T(8,128)S(1)} %get-tuple-element.194, f32[64]{0:T(128)S(1)} %mul.729, ...), kind=kLoop, calls=%fused_computation.7.clone.1 | loop fusion | flops 50331648 | bytes 29361152 | tf_op jit(solution)/shard_map/convert
  234.3 19.5 %fusion.52 = f32[8,64,128]{2,1,0:T(8,128)S(1)} fusion(f32[8,64,128]{2,1,0:T(8,128)S(1)} %get-tuple-element.219, s32[]{:T(128)} %get-tuple-element.218, bf16[128,131072]{1,0:T(8,128)(2,1)} %get-tuple-element.240, bf16[64,65536]{1,0:T(8,128)(2,1)} %get-tuple-element.201, bf16[64,65536]{1,0:T(8,128)(2,1)} %get-tuple-element.202), kind=kOutput, calls=%fused_computation.25.clone.1 | convolution fusion | flops 2181046272 | bytes 50364420 | tf_op jit(solution)/shard_map/while/body/eval_jaxpr/dot_general | solution.py:61
  255.7 8.6 %fusion.50 = (f32[8,65536]{1,0:T(8,128)S(1)}, f32[8,65536]{1,0:T(8,128)}) fusion(f32[65536]{0:T(1024)S(1)} %bitcast.169, f32[8]{0:T(128)S(1)} %get-tuple-element.186, f32[65536]{0:T(1024)S(1)} %bitcast.170, f32[8]{0:T(128)S(1)} %get-tuple-element.188, f32[65536]{0:T(1024)S(1)} %bitcast.168, f32[8]{0:T(128)S(1)} %get-tuple-element.190), kind=kLoop, calls=%fused_computation.18.clone.1 | loop fusion | flops 2621440 | bytes 4980832 | tf_op jit(solution)/shard_map/while/body/eval_jaxpr/cos | solution.py:34
  265.2 4.2 slice_bitcast_fusion.12
  269.4 8.9 %fusion.51 = (bf16[64,65536]{1,0:T(8,128)(2,1)}, bf16[64,65536]{1,0:T(8,128)(2,1)}) fusion(f32[8,65536]{1,0:T(8,128)S(1)} %get-tuple-element.191, f32[8,65536]{1,0:T(8,128)S(1)} %get-tuple-element.192, f32[64]{0:T(128)S(1)} %copy-done.5, f32[8,65536]{1,0:T(8,128)S(1)} %get-tuple-element.194, f32[64]{0:T(128)S(1)} %mul.729, ...), kind=kLoop, calls=%fused_computation.7.clone.1 | loop fusion | flops 50331648 | bytes 29361152 | tf_op jit(solution)/shard_map/convert
  278.3 19.5 %fusion.52 = f32[8,64,128]{2,1,0:T(8,128)S(1)} fusion(f32[8,64,128]{2,1,0:T(8,128)S(1)} %get-tuple-element.219, s32[]{:T(128)} %get-tuple-element.218, bf16[128,131072]{1,0:T(8,128)(2,1)} %get-tuple-element.240, bf16[64,65536]{1,0:T(8,128)(2,1)} %get-tuple-element.201, bf16[64,65536]{1,0:T(8,128)(2,1)} %get-tuple-element.202), kind=kOutput, calls=%fused_computation.25.clone.1 | convolution fusion | flops 2181046272 | bytes 50364420 | tf_op jit(solution)/shard_map/while/body/eval_jaxpr/dot_general | solution.py:61
  299.7 8.6 %fusion.50 = (f32[8,65536]{1,0:T(8,128)S(1)}, f32[8,65536]{1,0:T(8,128)}) fusion(f32[65536]{0:T(1024)S(1)} %bitcast.169, f32[8]{0:T(128)S(1)} %get-tuple-element.186, f32[65536]{0:T(1024)S(1)} %bitcast.170, f32[8]{0:T(128)S(1)} %get-tuple-element.188, f32[65536]{0:T(1024)S(1)} %bitcast.168, f32[8]{0:T(128)S(1)} %get-tuple-element.190), kind=kLoop, calls=%fused_computation.18.clone.1 | loop fusion | flops 2621440 | bytes 4980832 | tf_op jit(solution)/shard_map/while/body/eval_jaxpr/cos | solution.py:34
  309.2 4.2 slice_bitcast_fusion.12
  313.4 8.9 %fusion.51 = (bf16[64,65536]{1,0:T(8,128)(2,1)}, bf16[64,65536]{1,0:T(8,128)(2,1)}) fusion(f32[8,65536]{1,0:T(8,128)S(1)} %get-tuple-element.191, f32[8,65536]{1,0:T(8,128)S(1)} %get-tuple-element.192, f32[64]{0:T(128)S(1)} %copy-done.5, f32[8,65536]{1,0:T(8,128)S(1)} %get-tuple-element.194, f32[64]{0:T(128)S(1)} %mul.729, ...), kind=kLoop, calls=%fused_computation.7.clone.1 | loop fusion | flops 50331648 | bytes 29361152 | tf_op jit(solution)/shard_map/convert
  322.3 19.5 %fusion.52 = f32[8,64,128]{2,1,0:T(8,128)S(1)} fusion(f32[8,64,128]{2,1,0:T(8,128)S(1)} %get-tuple-element.219, s32[]{:T(128)} %get-tuple-element.218, bf16[128,131072]{1,0:T(8,128)(2,1)} %get-tuple-element.240, bf16[64,65536]{1,0:T(8,128)(2,1)} %get-tuple-element.201, bf16[64,65536]{1,0:T(8,128)(2,1)} %get-tuple-element.202), kind=kOutput, calls=%fused_computation.25.clone.1 | convolution fusion | flops 2181046272 | bytes 50364420 | tf_op jit(solution)/shard_map/while/body/eval_jaxpr/dot_general | solution.py:61
  343.7 8.6 %fusion.50 = (f32[8,65536]{1,0:T(8,128)S(1)}, f32[8,65536]{1,0:T(8,128)}) fusion(f32[65536]{0:T(1024)S(1)} %bitcast.169, f32[8]{0:T(128)S(1)} %get-tuple-element.186, f32[65536]{0:T(1024)S(1)} %bitcast.170, f32[8]{0:T(128)S(1)} %get-tuple-element.188, f32[65536]{0:T(1024)S(1)} %bitcast.168, f32[8]{0:T(128)S(1)} %get-tuple-element.190), kind=kLoop, calls=%fused_computation.18.clone.1 | loop fusion | flops 2621440 | bytes 4980832 | tf_op jit(solution)/shard_map/while/body/eval_jaxpr/cos | solution.py:34
  353.2 4.2 slice_bitcast_fusion.12
  357.3 8.9 %fusion.51 = (bf16[64,65536]{1,0:T(8,128)(2,1)}, bf16[64,65536]{1,0:T(8,128)(2,1)}) fusion(f32[8,65536]{1,0:T(8,128)S(1)} %get-tuple-element.191, f32[8,65536]{1,0:T(8,128)S(1)} %get-tuple-element.192, f32[64]{0:T(128)S(1)} %copy-done.5, f32[8,65536]{1,0:T(8,128)S(1)} %get-tuple-element.194, f32[64]{0:T(128)S(1)} %mul.729, ...), kind=kLoop, calls=%fused_computation.7.clone.1 | loop fusion | flops 50331648 | bytes 29361152 | tf_op jit(solution)/shard_map/convert
  366.3 19.5 %fusion.52 = f32[8,64,128]{2,1,0:T(8,128)S(1)} fusion(f32[8,64,128]{2,1,0:T(8,128)S(1)} %get-tuple-element.219, s32[]{:T(128)} %get-tuple-element.218, bf16[128,131072]{1,0:T(8,128)(2,1)} %get-tuple-element.240, bf16[64,65536]{1,0:T(8,128)(2,1)} %get-tuple-element.201, bf16[64,65536]{1,0:T(8,128)(2,1)} %get-tuple-element.202), kind=kOutput, calls=%fused_computation.25.clone.1 | convolution fusion | flops 2181046272 | bytes 50364420 | tf_op jit(solution)/shard_map/while/body/eval_jaxpr/dot_general | solution.py:61
  387.7 8.6 %fusion.50 = (f32[8,65536]{1,0:T(8,128)S(1)}, f32[8,65536]{1,0:T(8,128)}) fusion(f32[65536]{0:T(1024)S(1)} %bitcast.169, f32[8]{0:T(128)S(1)} %get-tuple-element.186, f32[65536]{0:T(1024)S(1)} %bitcast.170, f32[8]{0:T(128)S(1)} %get-tuple-element.188, f32[65536]{0:T(1024)S(1)} %bitcast.168, f32[8]{0:T(128)S(1)} %get-tuple-element.190), kind=kLoop, calls=%fused_computation.18.clone.1 | loop fusion | flops 2621440 | bytes 4980832 | tf_op jit(solution)/shard_map/while/body/eval_jaxpr/cos | solution.py:34
  397.2 4.2 slice_bitcast_fusion.12
  401.3 8.9 %fusion.51 = (bf16[64,65536]{1,0:T(8,128)(2,1)}, bf16[64,65536]{1,0:T(8,128)(2,1)}) fusion(f32[8,65536]{1,0:T(8,128)S(1)} %get-tuple-element.191, f32[8,65536]{1,0:T(8,128)S(1)} %get-tuple-element.192, f32[64]{0:T(128)S(1)} %copy-done.5, f32[8,65536]{1,0:T(8,128)S(1)} %get-tuple-element.194, f32[64]{0:T(128)S(1)} %mul.729, ...), kind=kLoop, calls=%fused_computation.7.clone.1 | loop fusion | flops 50331648 | bytes 29361152 | tf_op jit(solution)/shard_map/convert
  410.2 19.5 %fusion.52 = f32[8,64,128]{2,1,0:T(8,128)S(1)} fusion(f32[8,64,128]{2,1,0:T(8,128)S(1)} %get-tuple-element.219, s32[]{:T(128)} %get-tuple-element.218, bf16[128,131072]{1,0:T(8,128)(2,1)} %get-tuple-element.240, bf16[64,65536]{1,0:T(8,128)(2,1)} %get-tuple-element.201, bf16[64,65536]{1,0:T(8,128)(2,1)} %get-tuple-element.202), kind=kOutput, calls=%fused_computation.25.clone.1 | convolution fusion | flops 2181046272 | bytes 50364420 | tf_op jit(solution)/shard_map/while/body/eval_jaxpr/dot_general | solution.py:61
  430.5 2.4 collective-permute-start.2
  432.9 4.3 collective-permute-start.3
  437.9 1.4 fusion.39
  440.6 1.4 multiply_reduce_fusion.8
  443.3 5.5 %reduce-scatter.2.cloned.1.call-done = f32[128,128]{1,0:T(8,128)} async-done(((f32[512,128]{1,0:T(8,128)}), f32[128,128]{1,0:T(8,128)}) %reduce-scatter.2.cloned.1.call-update) | async-done | bytes 65552 | tf_op jit(solution)/shard_map/reduce_scatter | solution.py:149
  450.3 1.4 multiply_reduce_fusion.4
  452.3 17.7 %all-reduce = (f32[1]{0:T(128)}, f32[1,3,64]{2,0,1:T(1,128)S(1)}) all-reduce(f32[1]{0:T(128)} %bitcast.39, f32[1,3,64]{2,0,1:T(1,128)S(1)} %dynamic_update_slice.8), channel_id=1, replica_groups=mesh['image'=4,'band'=2,'ga'=4] {'band','ga'}, use_global_device_ids=true, to_apply=%region_13.14 | all-reduce | flops 193 | bytes 1544 | tf_op jit(solution)/shard_map/psum | solution.py:161
  470.7 4.7 collective-permute-start.1
  475.3 3.7 collective-permute-start
  484.5 1.4 multiply_reduce_fusion.5
  (205 shorter events, 23.4 us)
Async XLA Ops:
  7.2 441.6 %reduce-scatter.2.cloned.1.call-start = ((), (), s32[]{:S(2)}) async-start(), calls=%async_computation.1 | async-start | bytes 327680 | tf_op jit(solution)/shard_map/reduce_scatter | solution.py:149
  21.7 11.2 %copy-start.8 = (s32[64]{0:T(128)S(1)}, s32[64]{0:T(128)}, u32[]{:S(2)}) copy-start(s32[64]{0:T(128)} %param.20) | copy-start | bytes 772
  21.7 11.3 %copy-start.9 = (s32[4]{0:T(128)S(1)}, s32[4]{0:T(128)}, u32[]{:S(2)}) copy-start(s32[4]{0:T(128)} %param.21) | copy-start | bytes 52
  21.7 11.3 %copy-start.6 = (f32[1,3,64]{2,0,1:T(1,128)S(1)}, f32[1,3,64]{2,0,1:T(1,128)}, u32[]{:S(2)}) copy-start(f32[1,3,64]{2,0,1:T(1,128)} %param.23) | copy-start | bytes 2308
  21.7 11.3 %copy-start.7 = (f32[4,8]{1,0:T(4,128)S(1)}, f32[4,8]{1,0:T(4,128)}, u32[]{:S(2)}) copy-start(f32[4,8]{1,0:T(4,128)} %param.22) | copy-start | bytes 388
  45.3 32.6 %copy-start.1 = (f32[3,65536]{1,0:T(4,128)S(1)}, f32[3,65536]{1,0:T(4,128)}, u32[]{:S(2)}) copy-start(f32[3,65536]{1,0:T(4,128)} %param.19) | copy-start | bytes 2359300
  77.8 10.5 %copy-start.3 = (f32[3,64]{1,0:T(4,128)}, f32[3,64]{1,0:T(4,128)S(1)}, u32[]{:S(2)}) copy-start(f32[3,64]{1,0:T(4,128)S(1)} %get-tuple-element.238) | copy-start | bytes 2308 | tf_op jit(solution)/shard_map/while
  89.2 4.2 copy-start
  89.2 4.2 copy-start.5
  102.3 19.5 %copy-start.4 = (f32[3,64]{1,0:T(4,128)S(1)}, f32[3,64]{1,0:T(4,128)}, u32[]{:S(2)}) copy-start(f32[3,64]{1,0:T(4,128)} %copy-done.3) | copy-start | bytes 2308 | tf_op jit(solution)/shard_map/while
  102.3 19.5 %copy-start.11 = (s32[8]{0:T(128)S(1)}, s32[8]{0:T(128)}, u32[]{:S(2)}) copy-start(s32[8]{0:T(128)} %copy-done.10) | copy-start | bytes 100 | tf_op jit(solution)/shard_map/while
  121.8 10.5 %copy-start.3 = (f32[3,64]{1,0:T(4,128)}, f32[3,64]{1,0:T(4,128)S(1)}, u32[]{:S(2)}) copy-start(f32[3,64]{1,0:T(4,128)S(1)} %get-tuple-element.238) | copy-start | bytes 2308 | tf_op jit(solution)/shard_map/while
  133.2 4.2 copy-start
  133.2 4.2 copy-start.5
  146.3 19.5 %copy-start.4 = (f32[3,64]{1,0:T(4,128)S(1)}, f32[3,64]{1,0:T(4,128)}, u32[]{:S(2)}) copy-start(f32[3,64]{1,0:T(4,128)} %copy-done.3) | copy-start | bytes 2308 | tf_op jit(solution)/shard_map/while
  146.3 19.5 %copy-start.11 = (s32[8]{0:T(128)S(1)}, s32[8]{0:T(128)}, u32[]{:S(2)}) copy-start(s32[8]{0:T(128)} %copy-done.10) | copy-start | bytes 100 | tf_op jit(solution)/shard_map/while
  165.8 10.5 %copy-start.3 = (f32[3,64]{1,0:T(4,128)}, f32[3,64]{1,0:T(4,128)S(1)}, u32[]{:S(2)}) copy-start(f32[3,64]{1,0:T(4,128)S(1)} %get-tuple-element.238) | copy-start | bytes 2308 | tf_op jit(solution)/shard_map/while
  177.2 4.2 copy-start
  177.2 4.2 copy-start.5
  190.3 19.5 %copy-start.4 = (f32[3,64]{1,0:T(4,128)S(1)}, f32[3,64]{1,0:T(4,128)}, u32[]{:S(2)}) copy-start(f32[3,64]{1,0:T(4,128)} %copy-done.3) | copy-start | bytes 2308 | tf_op jit(solution)/shard_map/while
  190.3 19.5 %copy-start.11 = (s32[8]{0:T(128)S(1)}, s32[8]{0:T(128)}, u32[]{:S(2)}) copy-start(s32[8]{0:T(128)} %copy-done.10) | copy-start | bytes 100 | tf_op jit(solution)/shard_map/while
  209.8 10.5 %copy-start.3 = (f32[3,64]{1,0:T(4,128)}, f32[3,64]{1,0:T(4,128)S(1)}, u32[]{:S(2)}) copy-start(f32[3,64]{1,0:T(4,128)S(1)} %get-tuple-element.238) | copy-start | bytes 2308 | tf_op jit(solution)/shard_map/while
  221.2 4.2 copy-start
  221.2 4.2 copy-start.5
  234.3 19.5 %copy-start.4 = (f32[3,64]{1,0:T(4,128)S(1)}, f32[3,64]{1,0:T(4,128)}, u32[]{:S(2)}) copy-start(f32[3,64]{1,0:T(4,128)} %copy-done.3) | copy-start | bytes 2308 | tf_op jit(solution)/shard_map/while
  234.3 19.5 %copy-start.11 = (s32[8]{0:T(128)S(1)}, s32[8]{0:T(128)}, u32[]{:S(2)}) copy-start(s32[8]{0:T(128)} %copy-done.10) | copy-start | bytes 100 | tf_op jit(solution)/shard_map/while
  253.8 10.5 %copy-start.3 = (f32[3,64]{1,0:T(4,128)}, f32[3,64]{1,0:T(4,128)S(1)}, u32[]{:S(2)}) copy-start(f32[3,64]{1,0:T(4,128)S(1)} %get-tuple-element.238) | copy-start | bytes 2308 | tf_op jit(solution)/shard_map/while
  265.2 4.2 copy-start
  265.2 4.2 copy-start.5
  278.3 19.5 %copy-start.4 = (f32[3,64]{1,0:T(4,128)S(1)}, f32[3,64]{1,0:T(4,128)}, u32[]{:S(2)}) copy-start(f32[3,64]{1,0:T(4,128)} %copy-done.3) | copy-start | bytes 2308 | tf_op jit(solution)/shard_map/while
  278.3 19.5 %copy-start.11 = (s32[8]{0:T(128)S(1)}, s32[8]{0:T(128)}, u32[]{:S(2)}) copy-start(s32[8]{0:T(128)} %copy-done.10) | copy-start | bytes 100 | tf_op jit(solution)/shard_map/while
  297.8 10.5 %copy-start.3 = (f32[3,64]{1,0:T(4,128)}, f32[3,64]{1,0:T(4,128)S(1)}, u32[]{:S(2)}) copy-start(f32[3,64]{1,0:T(4,128)S(1)} %get-tuple-element.238) | copy-start | bytes 2308 | tf_op jit(solution)/shard_map/while
  309.2 4.2 copy-start
  309.2 4.2 copy-start.5
  322.3 19.5 %copy-start.4 = (f32[3,64]{1,0:T(4,128)S(1)}, f32[3,64]{1,0:T(4,128)}, u32[]{:S(2)}) copy-start(f32[3,64]{1,0:T(4,128)} %copy-done.3) | copy-start | bytes 2308 | tf_op jit(solution)/shard_map/while
  322.3 19.5 %copy-start.11 = (s32[8]{0:T(128)S(1)}, s32[8]{0:T(128)}, u32[]{:S(2)}) copy-start(s32[8]{0:T(128)} %copy-done.10) | copy-start | bytes 100 | tf_op jit(solution)/shard_map/while
  341.8 10.5 %copy-start.3 = (f32[3,64]{1,0:T(4,128)}, f32[3,64]{1,0:T(4,128)S(1)}, u32[]{:S(2)}) copy-start(f32[3,64]{1,0:T(4,128)S(1)} %get-tuple-element.238) | copy-start | bytes 2308 | tf_op jit(solution)/shard_map/while
  353.2 4.2 copy-start.5
  366.2 19.5 %copy-start.4 = (f32[3,64]{1,0:T(4,128)S(1)}, f32[3,64]{1,0:T(4,128)}, u32[]{:S(2)}) copy-start(f32[3,64]{1,0:T(4,128)} %copy-done.3) | copy-start | bytes 2308 | tf_op jit(solution)/shard_map/while
  366.2 19.5 %copy-start.11 = (s32[8]{0:T(128)S(1)}, s32[8]{0:T(128)}, u32[]{:S(2)}) copy-start(s32[8]{0:T(128)} %copy-done.10) | copy-start | bytes 100 | tf_op jit(solution)/shard_map/while
  385.8 10.5 %copy-start.3 = (f32[3,64]{1,0:T(4,128)}, f32[3,64]{1,0:T(4,128)S(1)}, u32[]{:S(2)}) copy-start(f32[3,64]{1,0:T(4,128)S(1)} %get-tuple-element.238) | copy-start | bytes 2308 | tf_op jit(solution)/shard_map/while
  397.1 4.2 copy-start.5
  410.2 19.5 %copy-start.4 = (f32[3,64]{1,0:T(4,128)S(1)}, f32[3,64]{1,0:T(4,128)}, u32[]{:S(2)}) copy-start(f32[3,64]{1,0:T(4,128)} %copy-done.3) | copy-start | bytes 2308 | tf_op jit(solution)/shard_map/while
  410.2 19.5 %copy-start.11 = (s32[8]{0:T(128)S(1)}, s32[8]{0:T(128)}, u32[]{:S(2)}) copy-start(s32[8]{0:T(128)} %copy-done.10) | copy-start | bytes 100 | tf_op jit(solution)/shard_map/while
  430.5 10.1 %collective-permute-start.2 = (f32[1,3,64]{2,0,1:T(1,128)}, f32[1,3,64]{2,0,1:T(1,128)S(1)}, u32[]{:S(2)}, u32[]{:S(2)}) collective-permute-start(f32[1,3,64]{2,0,1:T(1,128)} %param.23), channel_id=1, source_target_pairs={{8,0},{16,8},{24,16},{9,1},{17,9},{25,17},{10,2},{18,10},{26,18},{... | collective-permute-start | bytes 2312 | tf_op jit(solution)/shard_map/ppermute | solution.py:19
  432.9 7.7 %collective-permute-start.3 = (f32[1,3,64]{2,0,1:T(1,128)}, f32[1,3,64]{2,0,1:T(1,128)S(1)}, u32[]{:S(2)}, u32[]{:S(2)}) collective-permute-start(f32[1,3,64]{2,0,1:T(1,128)} %param.23), channel_id=1, source_target_pairs={{0,8},{8,16},{16,24},{1,9},{9,17},{17,25},{2,10},{10,18},{18,26},{... | collective-permute-start | bytes 2312 | tf_op jit(solution)/shard_map/ppermute | solution.py:19
  470.7 8.4 %collective-permute-start.1 = (f32[1]{0:T(128)}, f32[1]{0:T(128)}, u32[]{:S(2)}, u32[]{:S(2)}) collective-permute-start(f32[1]{0:T(128)} %add.109), channel_id=1, source_target_pairs={{0,8},{8,16},{16,24},{1,9},{9,17},{17,25},{2,10},{10,18},{18,26},{... | collective-permute-start | bytes 20 | tf_op jit(solution)/shard_map/ppermute | solution.py:19
  475.3 6.3 %collective-permute-start = (f32[1]{0:T(128)}, f32[1]{0:T(128)}, u32[]{:S(2)}, u32[]{:S(2)}) collective-permute-start(f32[1]{0:T(128)} %add.109), channel_id=1, source_target_pairs={{8,0},{16,8},{24,16},{9,1},{17,9},{25,17},{10,2},{18,10},{26,18},{... | collective-permute-start | bytes 20 | tf_op jit(solution)/shard_map/ppermute | solution.py:19
  (11 other events, 19.2 us)
Sparse Core Ops, SparseCore 0:
  430.6 18.1 reduce-scatter.1
where the time goes:
time: 497 us; the launch traced here: 496 us
  other arithmetic  196 us (39%)
  matrix products  156 us (31%)
  local copies, waits for them, and re-layouts  75.2 us (15%)
  between operations  23.4 us (5%)
  blocking collectives  17.7 us (4%)
  starting transfers between devices  15.2 us (3%)
  waiting for transfers between devices  6.81 us (1%)
  loops' own time  6.05 us (1%)
    dot_general x8, matrix products, contract(): lax.dot_general(projector, stacked, (((1,), (1,)), ((), ())), preferred_e...  156 us
    another operation x9, other arithmetic  82.8 us
    cos x8, other arithmetic, projectors(): cosine = jnp.cos(phases)  69.1 us
    mul x16, local copies, waits for them, and re-layouts, projectors(): radial = species_mask[:, 0, :, None] * form_factor[0][None, :, :]  33.8 us
    concatenate x1, other arithmetic, stack_waves(): return jnp.concatenate(pieces, axis=0)  32.5 us
    unnamed x15, local copies, waits for them, and re-layouts  23.1 us
    psum x1, blocking collectives, per_device(): force_nl, energy_nl = lax.psum((force_full, energy_part), ('band', 'ga'))  17.7 us
    ppermute x4, starting transfers between devices, passed_along(): return lax.ppermute(array, axis, pairs)  15.1 us
  transfers between devices with their start and end apart: 5, of which 2 were waited for; matrix products, arithmetic and copies ran while one was open for 1% of the time, Pallas kernels for 0%

commit v1 on v0

--- a/solution.py
+++ b/solution.py
@@ -3,6 +3,8 @@
 import jax
 import jax.numpy as jnp
 from jax import lax
+from jax.experimental import pallas as pl
+from jax.experimental.pallas import tpu as pltpu
 from jax.sharding import PartitionSpec as P
 
 ATOMS = 64
@@ -27,40 +29,137 @@
     return (species_mask, strength)
 
 
-def projectors(atom_pos, species_mask, form_factor, g_vectors):
-    phases = atom_pos[0][:, None] * g_vectors[0][None, :]
-    phases = phases + atom_pos[1][:, None] * g_vectors[1][None, :]
-    phases = phases + atom_pos[2][:, None] * g_vectors[2][None, :]
-    cosine = jnp.cos(phases)
-    sine_part = jnp.sin(phases)
-    radial = species_mask[:, 0, :, None] * form_factor[0][None, :, :]
-    for spec_num in range(1, SPECIES):
-        radial = radial + species_mask[:, spec_num, :, None] * form_factor[spec_num][None, :, :]
-    real_part = radial * cosine[:, None, :]
-    imag_part = -radial * sine_part[:, None, :]
-    joined = jnp.concatenate([real_part, imag_part], axis=-1).astype(jnp.bfloat16)
-    return joined.reshape(joined.shape[0] * joined.shape[1], joined.shape[2])
-
-
-def stack_waves(waves_here, g_vectors):
-    band_count = waves_here.shape[0]
-    real_part = waves_here[:, 0, :].astype(jnp.float32)
-    imag_part = waves_here[:, 1, :].astype(jnp.float32)
-    pieces = [waves_here.reshape(band_count, 2 * waves_here.shape[2])]
-    for axis_num in range(3):
-        direction = g_vectors[axis_num][None, :]
-        pieces.append(
-            jnp.concatenate([-direction * imag_part, direction * real_part], axis=-1).astype(
-                jnp.bfloat16
+SIN_HALF = (0.7071067780965931, -0.02946276693049568, 0.00036827213876565137, -2.1885830267998076e-06, 7.194201360627222e-09)
+COS_HALF = (-1.4142134949348355, 0.17677635430234293, -0.003682571658574129, 3.061195661905538e-05, -1.2786908538293617e-07)
+TURN_HIGH = 6.28125
+TURN_LOW = 0.001935307179586232
+ROUNDER = 12582912.0
+SUB = 1024
+BLOCK = 8192
+GROUP = 8
+
+
+def horner(coefs, z):
+    total = coefs[-1] * z + coefs[-2]
+    for coef in coefs[-3::-1]:
+        total = total * z + coef
+    return total
+
+
+def cos_and_minus_sin(phases):
+    turns = (phases * 0.15915494309189535 + ROUNDER) - ROUNDER
+    r = (phases - turns * TURN_HIGH) - turns * TURN_LOW
+    z = r * r
+    half_sin = r * horner(SIN_HALF, z)
+    return (1.0 - half_sin * half_sin, half_sin * horner(COS_HALF, z))
+
+
+def sums_kernel(spec_ref, w_ref, ff_ref, g_ref, pos_ref, live_ref, out_ref,
+                acc, rad, stk, prj, trig):
+    step = pl.program_id(0)
+    rows = w_ref.shape[0]
+    bands = rows // 2
+    block = w_ref.shape[1]
+    sub = stk.shape[1]
+    groups = prj.shape[0]
+    half = GROUP * PMAX
+
+    @pl.when(step == 0)
+    def _():
+        acc[...] = jnp.zeros_like(acc)
+
+    def wide(x):
+        return jnp.concatenate([x] * (sub // 128), axis=1)
+
+    def body(t, carry):
+        lanes = pl.ds(pl.multiple_of(t * sub, sub), sub)
+        for s in range(SPECIES):
+            rad[s] = ff_ref[s, :, lanes] * wide(live_ref[s])
+        w = w_ref[:, lanes]
+        stk[0:rows, :] = w
+        for c in range(3):
+            stk[(c + 1) * rows : (c + 2) * rows, :] = (
+                g_ref[c : c + 1, lanes] * w.astype(jnp.float32)
+            ).astype(jnp.bfloat16)
+
+        def multiply(j):
+            acc[j] += lax.dot_general(
+                prj[j], stk[...], (((1,), (1,)), ((), ())), preferred_element_type=jnp.float32
             )
-        )
-    return jnp.concatenate(pieces, axis=0)
-
-
-def contract(projector, stacked):
-    return 2.0 * lax.dot_general(
-        projector, stacked, (((1,), (1,)), ((), ())), preferred_element_type=jnp.float32
-    )
+
+        for j in range(groups):
+            mine = slice(j * GROUP, (j + 1) * GROUP)
+            phases = wide(pos_ref[0, mine, :]) * g_ref[0:1, lanes]
+            phases = phases + wide(pos_ref[1, mine, :]) * g_ref[1:2, lanes]
+            phases = phases + wide(pos_ref[2, mine, :]) * g_ref[2:3, lanes]
+            cosine, minus_sine = cos_and_minus_sin(phases)
+            trig[j, 0] = cosine
+            trig[j, 1] = minus_sine
+            for i in range(0, GROUP, 2):
+                first = rad[spec_ref[j * GROUP + i]]
+                second = rad[spec_ref[j * GROUP + i + 1]]
+                for part in range(2):
+                    pair = jnp.concatenate(
+                        [first * trig[j, part, i : i + 1, :],
+                         second * trig[j, part, i + 1 : i + 2, :]], axis=0)
+                    at = part * half + i * PMAX
+                    prj[j, at : at + 2 * PMAX, :] = pair.astype(jnp.bfloat16)
+            if j > 0:
+                multiply(j - 1)
+        multiply(groups - 1)
+        return carry
+
+    lax.fori_loop(0, block // sub, body, 0)
+
+    @pl.when(step == pl.num_programs(0) - 1)
+    def _():
+        for j in range(groups):
+            real = acc[j, :half, :]
+            imag = acc[j, half:, :]
+            here = slice(j * half, (j + 1) * half)
+            out_ref[here, 0:bands] = 2.0 * (real[:, :bands] + imag[:, bands:rows])
+            for c in range(1, 4):
+                out_ref[here, c * bands : (c + 1) * bands] = 2.0 * (
+                    imag[:, c * rows : c * rows + bands]
+                    - real[:, c * rows + bands : (c + 1) * rows]
+                )
+
+
+def projector_sums(waves, form_factor, g_vectors, species, proj_count, atom_pos):
+    bands, _, length = waves.shape
+    atoms = species.shape[0]
+    w = jnp.swapaxes(waves, 0, 1).reshape(2 * bands, length)
+    block = math.gcd(length, BLOCK)
+    sub = math.gcd(block, SUB)
+    groups = atoms // GROUP
+    live = (jnp.arange(PMAX)[None, :] < proj_count[:, None]).astype(jnp.float32)
+    live = jnp.broadcast_to(live[:, :, None], (SPECIES, PMAX, 128))
+    pos = jnp.broadcast_to(atom_pos[:, :, None], (3, atoms, 128))
+    grid_spec = pltpu.PrefetchScalarGridSpec(
+        num_scalar_prefetch=1,
+        grid=(length // block,),
+        in_specs=[
+            pl.BlockSpec((2 * bands, block), lambda i, sp: (0, i)),
+            pl.BlockSpec((SPECIES, PMAX, block), lambda i, sp: (0, 0, i)),
+            pl.BlockSpec((3, block), lambda i, sp: (0, i)),
+            pl.BlockSpec((3, atoms, 128), lambda i, sp: (0, 0, 0)),
+            pl.BlockSpec((SPECIES, PMAX, 128), lambda i, sp: (0, 0, 0)),
+        ],
+        out_specs=pl.BlockSpec((atoms * PMAX, 4 * bands), lambda i, sp: (0, 0)),
+        scratch_shapes=[
+            pltpu.VMEM((groups, 2 * GROUP * PMAX, 8 * bands), jnp.float32),
+            pltpu.VMEM((SPECIES, PMAX, sub), jnp.float32),
+            pltpu.VMEM((8 * bands, sub), jnp.bfloat16),
+            pltpu.VMEM((groups, 2 * GROUP * PMAX, sub), jnp.bfloat16),
+            pltpu.VMEM((groups, 2, GROUP, sub), jnp.float32),
+        ],
+    )
+    return pl.pallas_call(
+        sums_kernel,
+        grid_spec=grid_spec,
+        out_shape=jax.ShapeDtypeStruct((atoms * PMAX, 4 * bands), jnp.float32),
+        compiler_params=pltpu.CompilerParams(vmem_limit_bytes=48 * 1024 * 1024),
+    )(species, w, form_factor, g_vectors, pos, live)
 
 
 def nonlocal_terms(proj_sums, occupied, strength):
@@ -130,28 +229,12 @@
     tangent_kind,
 ):
     species_mask, strength = atom_tables(species, proj_count, coupling)
-    stacked = stack_waves(wave_coeffs[0], g_vectors)
-    atom_pos = positions[0]
     occupied = occupation[0]
     local_atoms = ATOMS // lax.axis_size("ga")
-    natoms = lax.axis_size("ga") * (local_atoms * PMAX) // PMAX
-    block_atoms = math.gcd(natoms, 8)
-    block_count = natoms // block_atoms
-
-    def one_block(block_num):
-        begin = block_num * block_atoms
-        pos_part = lax.dynamic_slice_in_dim(atom_pos, begin, block_atoms, 1)
-        mask_part = lax.dynamic_slice_in_dim(species_mask, begin, block_atoms, 0)
-        projector = projectors(pos_part, mask_part, form_factor, g_vectors)
-        return contract(projector, stacked)
-
-    blocks = lax.map(one_block, jnp.arange(block_count, dtype=jnp.int32))
-    proj_sums = lax.psum_scatter(
-        blocks.reshape(lax.axis_size("ga") * (local_atoms * PMAX), blocks.shape[2]),
-        "ga",
-        scatter_dimension=0,
-        tiled=True,
-    )
+    sums = projector_sums(
+        wave_coeffs[0], form_factor, g_vectors, species, proj_count, positions[0]
+    )
+    proj_sums = lax.psum_scatter(sums, "ga", scatter_dimension=0, tiled=True)
     first_local = lax.axis_index("ga") * local_atoms
     strength_part = lax.dynamic_slice_in_dim(strength, first_local, local_atoms, 0)
     energy_part, force_part = nonlocal_terms(proj_sums, occupied, strength_part)

time: 497 us -> 185 us (0.37)
  other arithmetic: 196 us -> 5.94 us
  matrix products: 156 us -> 0 us
  Pallas kernels: 0 us -> 94.8 us
  local copies, waits for them, and re-layouts: 75.2 us -> 14 us
  waiting for transfers between devices: 6.81 us -> 14 us
  loops' own time: 6.05 us -> 0 us
    dot_general x8 -> x0, matrix products: 156 us -> none  [contract(): lax.dot_general(projector, stacked, (((1,), (1,)), ((), ())), preferred_e...]
    pallas_call x0 -> x1, Pallas kernels: none -> 94.8 us  [projector_sums(): pl.pallas_call(sums_kernel, grid_spec=grid_spec, out_shape=jax.ShapeDtype...]
    another operation x9 -> x0, other arithmetic: 82.8 us -> none
    cos x8 -> x0, other arithmetic: 69.1 us -> none  [projectors(): cosine = jnp.cos(phases)]
    mul x48 -> x0, local copies, waits for them, and re-layouts: 39.9 us -> none  [the longest x16 33.8 us: projectors(): radial = species_mask[:, 0, :, None] * form_factor[0][None, :, :]]
    concatenate x1 -> x0, other arithmetic: 32.5 us -> none  [stack_waves(): return jnp.concatenate(pieces, axis=0)]
    unnamed x15 -> x17, local copies, waits for them, and re-layouts: 23.1 us -> 0.74 us
    transpose x0 -> x1, local copies, waits for them, and re-layouts: none -> 11.3 us  [projector_sums(): w = jnp.swapaxes(waves, 0, 1).reshape(2 * bands, length)]
  transfers between devices with their start and end apart: 5 -> 5, of which waited for: 2 -> 2; matrix products, arithmetic and copies ran while one was open for 1% -> 8% of each run, Pallas kernels for 0% -> 51%
where the time goes in v1:
time: 185 us
  Pallas kernels  94.8 us (51%)
  between operations  23.4 us (13%)
  blocking collectives  17.7 us (10%)
  starting transfers between devices  15.2 us (8%)
  local copies, waits for them, and re-layouts  14 us (8%)
  waiting for transfers between devices  14 us (8%)
  other arithmetic  5.94 us (3%)
    pallas_call x1, Pallas kernels, projector_sums(): pl.pallas_call(sums_kernel, grid_spec=grid_spec, out_shape=jax.ShapeDtype...  94.8 us
    psum x1, blocking collectives, per_device(): force_nl, energy_nl = lax.psum((force_full, energy_part), ('band', 'ga'))  17.7 us
    ppermute x4, starting transfers between devices, passed_along(): return lax.ppermute(array, axis, pairs)  15.1 us
    reduce_scatter x1, waiting for transfers between devices, per_device(): proj_sums = lax.psum_scatter(sums, 'ga', scatter_dimension=0, tiled=True)  12.6 us
    transpose x1, local copies, waits for them, and re-layouts, projector_sums(): w = jnp.swapaxes(waves, 0, 1).reshape(2 * bands, length)  11.3 us
  transfers between devices with their start and end apart: 5, of which 2 were waited for; matrix products, arithmetic and copies ran while one was open for 8% of the time, Pallas kernels for 51%

profile of v1, /device:TPU:10, one launch (start us, length us, event | category | flops | bytes accessed | tf_op | source)
XLA Modules:
  0.0 185.1 jit_solution(859380208025803431)
XLA Ops:
  7.2 0.0 reduce-scatter.2.cloned.1.call-start
  7.2 2.4 %collective-permute-start.2 = (f32[1,3,64]{2,0,1:T(1,128)}, f32[1,3,64]{2,0,1:T(1,128)S(1)}, u32[]{:S(2)}, u32[]{:S(2)}) collective-permute-start(f32[1,3,64]{2,0,1:T(1,128)} %param.21), channel_id=1, source_target_pairs={{8,0},{16,8},{24,16},{9,1},{17,9},{25,17},{10,2},{18,10},{26,18},{... | collective-permute-start | bytes 2312 | tf_op jit(solution)/shard_map/ppermute | solution.py:21
  9.7 4.3 %collective-permute-start.3 = (f32[1,3,64]{2,0,1:T(1,128)}, f32[1,3,64]{2,0,1:T(1,128)S(1)}, u32[]{:S(2)}, u32[]{:S(2)}) collective-permute-start(f32[1,3,64]{2,0,1:T(1,128)} %param.21), channel_id=1, source_target_pairs={{0,8},{8,16},{16,24},{1,9},{9,17},{17,25},{2,10},{10,18},{18,26},{... | collective-permute-start | bytes 2312 | tf_op jit(solution)/shard_map/ppermute | solution.py:21
  14.0 0.7 copy.28
  14.7 0.7 fusion.5
  15.4 11.3 %copy.20 = bf16[2,32,65536]{2,1,0:T(8,128)(2,1)} copy(bf16[2,32,65536]{2,0,1:T(2,128)(2,1)} %bitcast.30) | data formatting | bytes 16777216 | tf_op jit(solution)/shard_map/transpose | solution.py:131
  26.7 0.1 broadcast_in_dim.73.live_ref
  26.8 0.1 broadcast_in_dim.72.pos_ref
  26.8 0.0 copy-done
  26.9 0.0 copy-done.1
  26.9 0.0 copy-start.5
  26.9 0.0 copy-start.4
  26.9 0.0 copy-start.2
  26.9 0.0 copy-start.3
  26.9 0.0 copy-start.7
  26.9 0.0 copy-start.6
  26.9 94.8 %shard_map.149 = f32[512,128]{1,0:T(8,128)} custom-call(s32[64]{0:T(128)S(1)} %copy-done.1, bf16[64,65536]{1,0:T(8,128)(2,1)} %bitcast.29, f32[4,8,65536]{2,1,0:T(8,128)} %ff_ref.1, f32[3,65536]{1,0:T(4,128)S(1)} %copy-done, f32[3,64,128]{2,1,0:T(8,128)S(1)} %broadcast_in_dim.72.pos_ref, f32[4,8,128]{2,1,0:T(8,128)S(1)} %broadcast_in_dim.73.live_ref), custom_call_target="tpu_custom_call" | custom-call | tf_op jit(solution)/shard_map/pallas_call | solution.py:157
  121.8 0.0 reduce-scatter.2.cloned.1.call-update
  122.4 0.0 copy-done.5
  122.5 0.6 fusion.10
  123.1 0.0 copy-done.4
  123.1 0.1 multiply_reduce_fusion
  124.5 0.0 collective-permute-done.2
  124.5 0.0 collective-permute-done.3
  124.5 0.0 copy-done.2
  124.5 0.0 copy-done.3
  124.5 0.6 multiply_reduce_fusion.8
  126.5 12.6 %reduce-scatter.2.cloned.1.call-done = f32[128,128]{1,0:T(8,128)} async-done(((f32[512,128]{1,0:T(8,128)}), f32[128,128]{1,0:T(8,128)}) %reduce-scatter.2.cloned.1.call-update) | async-done | bytes 65552 | tf_op jit(solution)/shard_map/reduce_scatter | solution.py:237
  139.1 0.0 copy-done.7
  139.1 1.2 fusion
  140.3 0.1 reshape.172
  140.4 0.1 copy.21
  140.5 0.1 reshape.173
  140.6 0.1 copy.22
  140.7 0.1 reshape.174
  140.7 0.1 copy.23
  140.8 0.1 reduce_sum.127
  140.9 0.1 copy.25
  141.0 0.7 multiply_reduce_fusion.4
  141.7 0.5 dynamic_update_slice.4
  142.3 17.7 %all-reduce = (f32[1]{0:T(128)}, f32[1,3,64]{2,0,1:T(1,128)S(1)}) all-reduce(f32[1]{0:T(128)} %bitcast.12, f32[1,3,64]{2,0,1:T(1,128)S(1)} %dynamic_update_slice.4), channel_id=1, replica_groups=mesh['image'=4,'band'=2,'ga'=4] {'band','ga'}, use_global_device_ids=true, to_apply=%region_11.0 | all-reduce | flops 193 | bytes 1544 | tf_op jit(solution)/shard_map/psum | solution.py:244
  160.6 4.7 %collective-permute-start.1 = (f32[1]{0:T(128)}, f32[1]{0:T(128)}, u32[]{:S(2)}, u32[]{:S(2)}) collective-permute-start(f32[1]{0:T(128)} %add.67), channel_id=1, source_target_pairs={{0,8},{8,16},{16,24},{1,9},{9,17},{17,25},{2,10},{10,18},{18,26},{... | collective-permute-start | bytes 20 | tf_op jit(solution)/shard_map/ppermute | solution.py:21
  165.3 3.7 %collective-permute-start = (f32[1]{0:T(128)}, f32[1]{0:T(128)}, u32[]{:S(2)}, u32[]{:S(2)}) collective-permute-start(f32[1]{0:T(128)} %add.67), channel_id=1, source_target_pairs={{8,0},{16,8},{24,16},{9,1},{17,9},{25,17},{10,2},{18,10},{26,18},{... | collective-permute-start | bytes 20 | tf_op jit(solution)/shard_map/ppermute | solution.py:21
  170.2 1.4 collective-permute-done
  173.1 0.6 multiply_reduce_fusion.6
  174.4 0.0 copy-done.6
  174.5 0.7 multiply_reduce_fusion.5
  175.8 1.3 broadcast_select_fusion.5
  (9 shorter events, 0.0 us)
Async XLA Ops:
  7.2 132.0 %reduce-scatter.2.cloned.1.call-start = ((), (), s32[]{:S(2)}) async-start(), calls=%async_computation.1 | async-start | bytes 327680 | tf_op jit(solution)/shard_map/reduce_scatter | solution.py:237
  7.2 117.3 %collective-permute-start.2 = (f32[1,3,64]{2,0,1:T(1,128)}, f32[1,3,64]{2,0,1:T(1,128)S(1)}, u32[]{:S(2)}, u32[]{:S(2)}) collective-permute-start(f32[1,3,64]{2,0,1:T(1,128)} %param.21), channel_id=1, source_target_pairs={{8,0},{16,8},{24,16},{9,1},{17,9},{25,17},{10,2},{18,10},{26,18},{... | collective-permute-start | bytes 2312 | tf_op jit(solution)/shard_map/ppermute | solution.py:21
  9.7 114.8 %collective-permute-start.3 = (f32[1,3,64]{2,0,1:T(1,128)}, f32[1,3,64]{2,0,1:T(1,128)S(1)}, u32[]{:S(2)}, u32[]{:S(2)}) collective-permute-start(f32[1,3,64]{2,0,1:T(1,128)} %param.21), channel_id=1, source_target_pairs={{0,8},{8,16},{16,24},{1,9},{9,17},{17,25},{2,10},{10,18},{18,26},{... | collective-permute-start | bytes 2312 | tf_op jit(solution)/shard_map/ppermute | solution.py:21
  15.4 11.5 %copy-start = (f32[3,65536]{1,0:T(4,128)S(1)}, f32[3,65536]{1,0:T(4,128)}, u32[]{:S(2)}) copy-start(f32[3,65536]{1,0:T(4,128)} %g_ref.1) | copy-start | bytes 2359300
  15.4 11.5 %copy-start.1 = (s32[64]{0:T(128)S(1)}, s32[64]{0:T(128)}, u32[]{:S(2)}) copy-start(s32[64]{0:T(128)} %spec_ref.1) | copy-start | bytes 772
  26.9 95.6 %copy-start.5 = (f32[2]{0:T(128)S(1)}, f32[2]{0:T(128)}, u32[]{:S(2)}) copy-start(f32[2]{0:T(128)} %param.25) | copy-start | bytes 28
  26.9 96.2 %copy-start.4 = (f32[4,8]{1,0:T(4,128)S(1)}, f32[4,8]{1,0:T(4,128)}, u32[]{:S(2)}) copy-start(f32[4,8]{1,0:T(4,128)} %param.20) | copy-start | bytes 388
  26.9 97.6 %copy-start.2 = (f32[1,3,64]{2,0,1:T(1,128)S(1)}, f32[1,3,64]{2,0,1:T(1,128)}, u32[]{:S(2)}) copy-start(f32[1,3,64]{2,0,1:T(1,128)} %param.21) | copy-start | bytes 2308
  26.9 97.6 %copy-start.3 = (f32[2,3,64]{2,0,1:T(2,128)S(1)}, f32[2,3,64]{2,0,1:T(2,128)}, u32[]{:S(2)}) copy-start(f32[2,3,64]{2,0,1:T(2,128)} %param.24) | copy-start | bytes 4612
  26.9 112.2 %copy-start.7 = (f32[1,32]{1,0:T(1,128)S(1)}, f32[1,32]{1,0:T(1,128)}, u32[]{:S(2)}) copy-start(f32[1,32]{1,0:T(1,128)} %param.15) | copy-start | bytes 388
  26.9 147.5 %copy-start.6 = (f32[1,3,64]{2,0,1:T(1,128)S(1)}, f32[1,3,64]{2,0,1:T(1,128)}, u32[]{:S(2)}) copy-start(f32[1,3,64]{2,0,1:T(1,128)} %param.23) | copy-start | bytes 2308
  160.6 8.4 %collective-permute-start.1 = (f32[1]{0:T(128)}, f32[1]{0:T(128)}, u32[]{:S(2)}, u32[]{:S(2)}) collective-permute-start(f32[1]{0:T(128)} %add.67), channel_id=1, source_target_pairs={{0,8},{8,16},{16,24},{1,9},{9,17},{17,25},{2,10},{10,18},{18,26},{... | collective-permute-start | bytes 20 | tf_op jit(solution)/shard_map/ppermute | solution.py:21
  165.3 6.3 %collective-permute-start = (f32[1]{0:T(128)}, f32[1]{0:T(128)}, u32[]{:S(2)}, u32[]{:S(2)}) collective-permute-start(f32[1]{0:T(128)} %add.67), channel_id=1, source_target_pairs={{8,0},{16,8},{24,16},{9,1},{17,9},{25,17},{10,2},{18,10},{26,18},{... | collective-permute-start | bytes 20 | tf_op jit(solution)/shard_map/ppermute | solution.py:21
Sparse Core Ops, SparseCore 0:
  121.9 17.1 reduce-scatter.1
